TPU v7x, 128 devices: a whole 4x4x4 slice. The times are simulated.
128 devices in a mesh: replica: 1, dp: 128 (over z, y, x, core).
Axes of the slice: x: 4, y: 4, z: 4, core: 2. Of those that a mesh axis runs over, the one named last changes fastest.
Arguments:
- x: bfloat16 [512, 896], P(('replica', 'dp'))
- lengths: int32 [512], P(('replica', 'dp'))
- cache: bfloat16 [2, 512, 512, 576], P(None, ('replica', 'dp'))
- w_q: bfloat16 [2, 896, 9216], replicated
- w_o: bfloat16 [2, 8192, 896], replicated
- expert_ids: int32 [2, 512, 8], P(None, ('replica', 'dp'))
- slots: int32 [2, 512, 8], P(None, ('replica', 'dp'))
- route_w: float32 [2, 512, 8], P(None, ('replica', 'dp'))
- w1_exp: bfloat16 [2, 256, 896, 256], P(None, 'dp')
- w3_exp: bfloat16 [2, 256, 896, 256], P(None, 'dp')
- w2_exp: bfloat16 [2, 256, 256, 896], P(None, 'dp')
- w1_sh: bfloat16 [2, 896, 256], P(None, None, 'dp')
- w3_sh: bfloat16 [2, 896, 256], P(None, None, 'dp')
- w2_sh: bfloat16 [2, 256, 896], P(None, 'dp')
Outputs:
- output: bfloat16 [512, 896], P(('replica', 'dp'))
All inputs are finite; a program needn't handle non-finite values.
Results may differ from a plain program's by a relative error of at most 0.02.
Values are sent between devices in bfloat16 or wider.
A program may use at most 1 GiB of HBM per device.

v0:
```python
import jax
import jax.numpy as jnp
from jax import lax
from jax.sharding import PartitionSpec as P

NORM_EPS = 1e-6
ATT_SCALE = 1.0 / (192.0 ** 0.5)
LATENT = 512


def rms_norm(values):
    vals32 = values.astype(jnp.float32)
    return vals32 * lax.rsqrt(jnp.mean(vals32 * vals32, axis=-1, keepdims=True) + NORM_EPS)


def gated_hidden(tok_in, w_up, w_gate):
    gate_in = jnp.dot(tok_in, w_gate, preferred_element_type=jnp.float32)
    up_in = jnp.dot(tok_in, w_up, preferred_element_type=jnp.float32)
    return (jax.nn.silu(gate_in) * up_in).astype(jnp.bfloat16)


def local_attention(resid, lengths, cache_l, w_q_l, w_o_l):
    tok_count = resid.shape[0]
    seq_len, kv_dim = cache_l.shape[1], cache_l.shape[2]
    num_heads = w_q_l.shape[1] // kv_dim
    normed = rms_norm(resid).astype(jnp.bfloat16)
    queries = jnp.dot(normed, w_q_l, preferred_element_type=jnp.float32).astype(jnp.bfloat16)
    queries = queries.reshape(tok_count, num_heads, kv_dim)
    scores = jnp.einsum('bhc,btc->bht', queries, cache_l, preferred_element_type=jnp.float32) * ATT_SCALE
    valid = jnp.arange(seq_len)[None, None, :] < lengths[:, None, None]
    probs = jax.nn.softmax(jnp.where(valid, scores, -jnp.inf), axis=-1).astype(jnp.bfloat16)
    attn = jnp.einsum('bht,btc->bhc', probs, cache_l[:, :, :LATENT], preferred_element_type=jnp.float32)
    attn = attn.astype(jnp.bfloat16).reshape(tok_count, num_heads * LATENT)
    return (resid.astype(jnp.float32) + jnp.dot(attn, w_o_l, preferred_element_type=jnp.float32)).astype(jnp.bfloat16)


def route_select(ids_l, slot_l, experts, capacity):
    buf_rows = jnp.where(slot_l >= 0, ids_l * capacity + slot_l, -1)
    return (buf_rows[:, :, None] == jnp.arange(experts * capacity)).astype(jnp.bfloat16)


def solution(mesh):
    group = mesh.shape['dp']
    tok_axes = ('replica', 'dp')
    in_specs = (
        P(tok_axes, None), P(tok_axes), P(None, tok_axes, None, None),
        P(None, None, None), P(None, None, None),
        P(None, tok_axes, None), P(None, tok_axes, None), P(None, tok_axes, None),
        P(None, 'dp', None, None), P(None, 'dp', None, None), P(None, 'dp', None, None),
        P(None, None, 'dp'), P(None, None, 'dp'), P(None, 'dp', None),
    )

    def device_step(x, lengths, cache, w_q, w_o, expert_ids, slots, route_w, w1_exp, w3_exp, w2_exp, w1_sh, w3_sh, w2_sh):
        batch_dev, d_model = x.shape
        local_experts = w1_exp.shape[1]
        experts = local_experts * group
        top_k = expert_ids.shape[2]
        capacity = max(1, (2 * batch_dev * top_k) // experts)
        resid = x
        for layer_idx in range(cache.shape[0]):
            resid = local_attention(resid, lengths, cache[layer_idx], w_q[layer_idx], w_o[layer_idx])
            ffn_in = rms_norm(resid).astype(jnp.bfloat16)
            gathered = lax.all_gather(ffn_in, 'dp', axis=0, tiled=True)
            shared_h = gated_hidden(gathered, w1_sh[layer_idx], w3_sh[layer_idx])
            shared_part = jnp.dot(shared_h, w2_sh[layer_idx], preferred_element_type=jnp.float32)
            shared_out = lax.psum_scatter(shared_part, 'dp', scatter_dimension=0, tiled=True)
            select = route_select(expert_ids[layer_idx], slots[layer_idx], experts, capacity)
            dispatch = jnp.sum(select, axis=1)
            send_buf = jnp.einsum('br,bd->rd', dispatch, ffn_in, preferred_element_type=jnp.float32).astype(jnp.bfloat16)
            send_buf = send_buf.reshape(group, local_experts, capacity, d_model)
            recv_buf = lax.all_to_all(send_buf, 'dp', 0, 0, tiled=True)
            gate_in = jnp.einsum('sncd,ndf->nscf', recv_buf, w3_exp[layer_idx], preferred_element_type=jnp.float32)
            up_in = jnp.einsum('sncd,ndf->nscf', recv_buf, w1_exp[layer_idx], preferred_element_type=jnp.float32)
            hidden = (jax.nn.silu(gate_in) * up_in).astype(jnp.bfloat16)
            expert_out = jnp.einsum('nscf,nfd->sncd', hidden, w2_exp[layer_idx], preferred_element_type=jnp.float32).astype(jnp.bfloat16)
            returned = lax.all_to_all(expert_out, 'dp', 0, 0, tiled=True)
            returned = returned.reshape(experts * capacity, d_model)
            picked = jnp.einsum('cls,se->cle', select, returned, preferred_element_type=jnp.float32)
            routed = jnp.sum(route_w[layer_idx][:, :, None] * picked, axis=1)
            resid = (resid.astype(jnp.float32) + routed + shared_out).astype(jnp.bfloat16)
        return resid

    return jax.shard_map(device_step, mesh=mesh, in_specs=in_specs, out_specs=P(tok_axes, None), check_vma=False)
```

profile of v0, /device:TPU:1, one launch (start us, length us, event | category | flops | bytes accessed | tf_op | source)
XLA Modules:
  0.0 461.3 jit_solution(9462053922042228177)
XLA Ops:
  6.5 4.1 slice_bitcast_fusion.1
  10.8 8.0 %fusion.14 = bf16[4,9216]{1,0:T(4,128)(2,1)S(1)} fusion(bf16[2,896,9216]{2,1,0:T(8,128)(2,1)} %param.17, bf16[4,896]{1,0:T(4,128)(2,1)S(1)} %copy-done.1, f32[4]{0:T(128)S(1)} %add_rsqrt_fusion.3), kind=kOutput, calls=%fused_computation.14 | convolution fusion | flops 66107904 | bytes 16595984 | tf_op jit(solution)/shard_map/dot_general | solution.py:27
  19.0 2.3 fusion.163
  21.3 0.7 fusion.43
  22.0 6.4 %multiply_reduce_fusion.1 = (f32[4]{0:T(128)S(1)}, f32[4,896]{1,0:T(4,128)S(1)}) fusion(bf16[4,8192]{1,0:T(4,128)(2,1)S(1)} %bitcast.143, bf16[2,8192,896]{2,1,0:T(8,128)(2,1)} %param.18, bf16[4,896]{1,0:T(4,128)(2,1)S(1)} %copy-done.1), kind=kOutput, calls=%fused_computation.121 | convolution fusion | flops 58741756 | bytes 14767120 | tf_op jit(solution)/shard_map/dot_general | solution.py:34
  28.6 0.4 convolution_convert_fusion.3
  29.0 0.9 reshape.157
  29.9 11.5 %all-to-all-start = ((bf16[128,2,1,896]{3,1,2,0:T(2,128)(2,1)}), bf16[128,2,1,896]{3,1,2,0:T(2,128)(2,1)S(1)}, u32[]{:S(2)}, u32[]{:S(2)}) async-start(bf16[128,2,1,896]{3,1,2,0:T(2,128)(2,1)} %bitcast.5), calls=%async_computation | async-start | bytes 917504 | tf_op jit(solution)/shard_map/all_to_all | solution.py:71
  41.5 38.0 %all-gather = bf16[128,4,896]{2,1,0:T(4,128)(2,1)S(1)} all-gather(bf16[1,4,896]{2,1,0:T(4,128)(2,1)S(1)} %fusion.160), channel_id=1, replica_groups=mesh['replica'=1,'dp'=128] {'dp'}, dimensions={0}, use_global_device_ids=true | all-gather | bytes 924672 | tf_op jit(solution)/shard_map/all_gather | solution.py:63
  79.7 0.3 fusion.144
  80.1 2.1 fusion.69
  82.5 2.0 fusion.24
  84.6 1.2 copy.28
  85.8 5.6 %all-to-all-start.1 = ((bf16[128,2,1,896]{3,1,2,0:T(2,128)(2,1)}), bf16[128,2,1,896]{3,1,2,0:T(2,128)(2,1)S(1)}, u32[]{:S(2)}, u32[]{:S(2)}) async-start(bf16[128,2,1,896]{3,1,2,0:T(2,128)(2,1)} %copy.28), calls=%async_computation.1 | async-start | bytes 917504 | tf_op jit(solution)/shard_map/all_to_all | solution.py:76
  91.5 13.3 %all-to-all-done.1 = bf16[128,2,1,896]{3,1,2,0:T(2,128)(2,1)S(1)} async-done(((bf16[128,2,1,896]{3,1,2,0:T(2,128)(2,1)}), bf16[128,2,1,896]{3,1,2,0:T(2,128)(2,1)S(1)}, u32[]{:S(2)}, u32[]{:S(2)}) %all-to-all-start.1) | async-done | bytes 458784 | tf_op jit(solution)/shard_map/all_to_all | solution.py:76
  105.1 127.4 %all-reduce.5.cloned.1.call-done = f32[512,896]{1,0:T(8,128)} async-done(((f32[512,896]{1,0:T(8,128)}), f32[512,896]{1,0:T(8,128)}) %all-reduce.5.cloned.1.call-update) | async-done | bytes 1835024
  232.6 0.9 fusion.122
  233.5 8.0 %fusion.17 = bf16[4,9216]{1,0:T(4,128)(2,1)S(1)} fusion(bf16[2,896,9216]{2,1,0:T(8,128)(2,1)} %param.17, bf16[4,896]{1,0:T(4,128)(2,1)S(1)} %get-tuple-element.6, f32[4]{0:T(128)S(1)} %add_rsqrt_fusion.1), kind=kOutput, calls=%fused_computation.15 | convolution fusion | flops 66107904 | bytes 16595984 | tf_op jit(solution)/shard_map/dot_general | solution.py:27
  241.6 2.4 fusion.164
  244.0 0.7 fusion.40
  244.7 6.4 %multiply_reduce_fusion = (f32[4]{0:T(128)S(1)}, f32[4,896]{1,0:T(4,128)S(1)}) fusion(bf16[4,8192]{1,0:T(4,128)(2,1)S(1)} %bitcast.142, bf16[2,8192,896]{2,1,0:T(8,128)(2,1)} %param.18, bf16[4,896]{1,0:T(4,128)(2,1)S(1)} %get-tuple-element.6), kind=kOutput, calls=%fused_computation.119 | convolution fusion | flops 58741756 | bytes 14767120 | tf_op jit(solution)/shard_map/dot_general | solution.py:34
  251.2 35.0 %all-gather.1 = bf16[128,4,896]{2,1,0:T(4,128)(2,1)S(1)} all-gather(bf16[1,4,896]{2,1,0:T(4,128)(2,1)S(1)} %fusion.161), channel_id=1, replica_groups=mesh['replica'=1,'dp'=128] {'dp'}, dimensions={0}, use_global_device_ids=true | all-gather | bytes 924672 | tf_op jit(solution)/shard_map/all_gather | solution.py:63
  286.4 0.4 convolution_convert_fusion.2
  286.8 0.9 reshape.162
  287.8 5.4 %all-to-all-start.2 = ((bf16[128,2,1,896]{3,1,2,0:T(2,128)(2,1)}), bf16[128,2,1,896]{3,1,2,0:T(2,128)(2,1)S(1)}, u32[]{:S(2)}, u32[]{:S(2)}) async-start(bf16[128,2,1,896]{3,1,2,0:T(2,128)(2,1)} %bitcast.22), calls=%async_computation.2 | async-start | bytes 917504 | tf_op jit(solution)/shard_map/all_to_all | solution.py:71
  293.6 2.1 fusion.68
  295.7 10.2 %all-to-all-done.2 = bf16[128,2,1,896]{3,1,2,0:T(2,128)(2,1)S(1)} async-done(((bf16[128,2,1,896]{3,1,2,0:T(2,128)(2,1)}), bf16[128,2,1,896]{3,1,2,0:T(2,128)(2,1)S(1)}, u32[]{:S(2)}, u32[]{:S(2)}) %all-to-all-start.2) | async-done | bytes 458784 | tf_op jit(solution)/shard_map/all_to_all | solution.py:71
  306.2 2.0 fusion.25
  308.3 0.5 copy.32
  308.7 18.0 %all_to_all.20 = bf16[128,2,1,896]{3,1,2,0:T(2,128)(2,1)S(1)} all-to-all(bf16[128,2,1,896]{3,1,2,0:T(2,128)(2,1)S(1)} %copy.32), channel_id=1, replica_groups=mesh['replica'=1,'dp'=128] {'dp'}, dimensions={0} | all-to-all | bytes 917504 | tf_op jit(solution)/shard_map/all_to_all | solution.py:76
  327.2 125.9 %all-reduce.7.cloned.1.call-done = f32[512,896]{1,0:T(8,128)} async-done(((f32[512,896]{1,0:T(8,128)}), f32[512,896]{1,0:T(8,128)}) %all-reduce.7.cloned.1.call-update) | async-done | bytes 1835024
  453.1 1.4 fusion.124
  (51 shorter events, 3.3 us)
Async XLA Ops:
  6.5 4.1 copy-start.1
  10.8 8.1 %copy-start.8 = (s32[4]{0:T(128)S(1)}, s32[4]{0:T(128)}, u32[]{:S(2)}) copy-start(s32[4]{0:T(128)} %param.15) | copy-start | bytes 52
  22.0 6.4 %copy-start.5 = (s32[2,4,8]{2,1,0:T(4,128)S(1)}, s32[2,4,8]{2,1,0:T(4,128)}, u32[]{:S(2)}) copy-start(s32[2,4,8]{2,1,0:T(4,128)} %param.19) | copy-start | bytes 772
  22.0 6.4 %copy-start.6 = (s32[2,4,8]{2,1,0:T(4,128)S(1)}, s32[2,4,8]{2,1,0:T(4,128)}, u32[]{:S(2)}) copy-start(s32[2,4,8]{2,1,0:T(4,128)} %param.20) | copy-start | bytes 772
  28.9 50.8 %copy-start.4 = (bf16[2,896,2]{1,2,0:T(2,128)(2,1)S(1)}, bf16[2,896,2]{1,2,0:T(2,128)(2,1)}, u32[]{:S(2)}) copy-start(bf16[2,896,2]{1,2,0:T(2,128)(2,1)} %param.26) | copy-start | bytes 21508
  29.9 50.2 %copy-start.2 = (bf16[2,2,896]{2,1,0:T(2,128)(2,1)S(1)}, bf16[2,2,896]{2,1,0:T(2,128)(2,1)}, u32[]{:S(2)}) copy-start(bf16[2,2,896]{2,1,0:T(2,128)(2,1)} %param.27) | copy-start | bytes 21508
  29.9 50.2 %copy-start.3 = (bf16[2,896,2]{1,2,0:T(2,128)(2,1)S(1)}, bf16[2,896,2]{1,2,0:T(2,128)(2,1)}, u32[]{:S(2)}) copy-start(bf16[2,896,2]{1,2,0:T(2,128)(2,1)} %param.25) | copy-start | bytes 21508
  29.9 52.3 %all-to-all-start = ((bf16[128,2,1,896]{3,1,2,0:T(2,128)(2,1)}), bf16[128,2,1,896]{3,1,2,0:T(2,128)(2,1)S(1)}, u32[]{:S(2)}, u32[]{:S(2)}) async-start(bf16[128,2,1,896]{3,1,2,0:T(2,128)(2,1)} %bitcast.5), calls=%async_computation | async-start | bytes 917504 | tf_op jit(solution)/shard_map/all_to_all | solution.py:71
  41.4 191.2 %all-reduce.5.cloned.1.call-start = ((), (), s32[]{:S(2)}) async-start(), calls=%async_computation.4 | async-start | bytes 3670016
  80.1 2.2 copy-start.9
  82.5 8.9 %copy-start.7 = (f32[2,4,8]{2,1,0:T(4,128)S(1)}, f32[2,4,8]{2,1,0:T(4,128)}, u32[]{:S(2)}) copy-start(f32[2,4,8]{2,1,0:T(4,128)} %param.21) | copy-start | bytes 772
  85.8 18.9 %all-to-all-start.1 = ((bf16[128,2,1,896]{3,1,2,0:T(2,128)(2,1)}), bf16[128,2,1,896]{3,1,2,0:T(2,128)(2,1)S(1)}, u32[]{:S(2)}, u32[]{:S(2)}) async-start(bf16[128,2,1,896]{3,1,2,0:T(2,128)(2,1)} %copy.28), calls=%async_computation.1 | async-start | bytes 917504 | tf_op jit(solution)/shard_map/all_to_all | solution.py:76
  241.4 2.6 copy-start
  287.8 18.2 %all-to-all-start.2 = ((bf16[128,2,1,896]{3,1,2,0:T(2,128)(2,1)}), bf16[128,2,1,896]{3,1,2,0:T(2,128)(2,1)S(1)}, u32[]{:S(2)}, u32[]{:S(2)}) async-start(bf16[128,2,1,896]{3,1,2,0:T(2,128)(2,1)} %bitcast.22), calls=%async_computation.2 | async-start | bytes 917504 | tf_op jit(solution)/shard_map/all_to_all | solution.py:71
  293.2 159.9 %all-reduce.7.cloned.1.call-start = ((), (), s32[]{:S(2)}) async-start(), calls=%async_computation.5 | async-start | bytes 3670016
  293.6 12.3 %copy-start.10 = (bf16[2,2,896,256]{3,2,1,0:T(8,128)(2,1)S(1)}, bf16[2,2,896,256]{3,2,1,0:T(8,128)(2,1)}, u32[]{:S(2)}) copy-start(bf16[2,2,896,256]{3,2,1,0:T(8,128)(2,1)} %param.23) | copy-start | bytes 5505028
Sparse Core Ops, SparseCore 0:
  82.3 150.2 all-reduce.4
  298.9 154.1 all-reduce.6
where the time goes:
time: 462 us; the launch traced here: 461 us
  waiting for transfers between devices  277 us (60%)
  blocking collectives  91 us (20%)
  matrix products  45.5 us (10%)
  starting transfers between devices  22.6 us (5%)
  between operations  13.7 us (3%)
  local copies, waits for them, and re-layouts  8.91 us (2%)
    unnamed x4, waiting for transfers between devices  253 us
    all_gather x2, blocking collectives, device_step(): gathered = lax.all_gather(ffn_in, 'dp', axis=0, tiled=True)  73 us
    all_to_all x1, blocking collectives, device_step(): returned = lax.all_to_all(expert_out, 'dp', 0, 0, tiled=True)  18 us
    all_to_all x2, starting transfers between devices, device_step(): recv_buf = lax.all_to_all(send_buf, 'dp', 0, 0, tiled=True)  16.9 us
    dot_general x2, matrix products, local_attention(): jnp.dot(normed, w_q_l, preferred_element_type=jnp.float32)  16 us
    all_to_all x1, waiting for transfers between devices, device_step(): returned = lax.all_to_all(expert_out, 'dp', 0, 0, tiled=True)  13.3 us
    dot_general x2, matrix products, local_attention(): jnp.dot(attn, w_o_l, preferred_element_type=jnp.float32)  12.8 us
    all_to_all x2, waiting for transfers between devices, device_step(): recv_buf = lax.all_to_all(send_buf, 'dp', 0, 0, tiled=True)  10.2 us
  transfers between devices with their start and end apart: 5, of which 4 were waited for; matrix products, arithmetic and copies ran while one was open for 3% of the time, Pallas kernels for 0%

commit v1 on v0

v1 whole, which is shorter than its diff:
```python
import functools

import jax
import jax.numpy as jnp
from jax import lax
from jax.experimental import pallas as pl
from jax.experimental.pallas import tpu as pltpu
from jax.sharding import PartitionSpec as P

NORM_EPS = 1e-6
ATT_SCALE = 1.0 / (192.0 ** 0.5)
BF = jnp.bfloat16
F32 = jnp.float32
MESH = pl.DeviceIdType.MESH
DEPTH = 5


def grid_of(group):
    return (4, 4, group // 32, 2) if group >= 32 else (1, 1, group // 2, 2)


def rms(v):
    return v * lax.rsqrt(jnp.mean(v * v, axis=-1, keepdims=True) + NORM_EPS)


def nt_dot(a, b):
    return lax.dot_general(a, b, (((1,), (1,)), ((), ())), preferred_element_type=F32)


def dot(a, b):
    return jnp.dot(a, b, preferred_element_type=F32)


def kernel(
    group, nq, no,
    x_in, len_in, kv_in, wq_in, wo_in, ids_in, slot_in, rw_in, w1_in, w3_in, w2_in, w1s_in, w3s_in, w2s_in,
    out_ref,
    xb, len_s, ids_s, slot_s, rw_s, kv, wq, wo, w1, w3, w2, pack, sw,
    disp_out, disp_in, ret_out, ret_in, size, qflat, qs, osc, sel, place, gates,
    small_sem, kv_sem, wq_sem, wo_sem, ex_sem, pack_sem,
    ws_sem, wr_sem, fs_sem, fr_sem, ds_sem, dr_sem, rs_sem, rr_sem,
):
    layers, batch, kv_dim, seq = kv.shape
    d_model = xb.shape[1]
    heads = qs.shape[0]
    latent = osc.shape[2]
    top_k = ids_s.shape[2]
    experts = disp_out.shape[1]
    zs, ys, xs, cs = grid_of(group)
    half = group // cs * 2
    q_cols = wq.shape[2]
    o_rows = wo.shape[1]

    me = lax.axis_index("dp")
    my_core = me % cs
    my_x = (me // cs) % xs
    my_y = (me // (cs * xs)) % ys
    my_z = me // (cs * xs * ys)
    chip = me // cs

    def peer(i):
        core = (my_core + i) % cs
        px = (my_x + i // cs) % xs
        py = (my_y + i // (cs * xs)) % ys
        pz = (my_z + i // (cs * xs * ys)) % zs
        return ((pz * ys + py) * xs + px) * cs + core

    smalls = [
        pltpu.make_async_copy(src, dst, small_sem.at[i])
        for i, (src, dst) in enumerate(
            ((x_in, xb), (len_in, len_s), (ids_in, ids_s), (slot_in, slot_s), (rw_in, rw_s))
        )
    ]
    packs = [pltpu.make_async_copy(src, pack.at[:, i], pack_sem.at[i]) for i, src in enumerate((w1s_in, w3s_in, w2s_in))]

    def q_copy(layer, c):
        return pltpu.make_async_copy(wq_in.at[layer, :, pl.ds(c * q_cols, q_cols)], wq.at[c], wq_sem.at[c])

    def o_copy(layer, c):
        return pltpu.make_async_copy(wo_in.at[layer, pl.ds(c * o_rows, o_rows)], wo.at[c], wo_sem.at[c])

    def kv_copy(layer, b):
        return pltpu.make_async_copy(kv_in.at[layer, b], kv.at[layer, b], kv_sem.at[layer, b])

    def ex_copies(layer):
        return [
            pltpu.make_async_copy(src.at[layer], dst.at[layer], ex_sem.at[layer, i])
            for i, (src, dst) in enumerate(((w3_in, w3), (w1_in, w1), (w2_in, w2)))
        ]

    for cp in smalls:
        cp.start()
    stream = [q_copy(0, c) for c in range(nq)] + [kv_copy(0, b) for b in range(batch)]
    stream += [o_copy(0, c) for c in range(no)] + ex_copies(0)
    issued = [0]

    def issue(n):
        for _ in range(n):
            if issued[0] < len(stream):
                stream[issued[0]].start()
                issued[0] += 1

    issue(DEPTH)
    for cp in packs:
        cp.start()

    barrier = pltpu.get_barrier_semaphore()

    def signal(i, carry):
        pl.semaphore_signal(barrier, inc=1, device_id={"dp": peer(i)}, device_id_type=MESH)
        return carry

    lax.fori_loop(1, group, signal, 0)

    for cp in smalls:
        cp.wait()
    pairs = batch * top_k
    row = lax.broadcasted_iota(jnp.int32, (pairs, 1), 0)
    grow = lax.broadcasted_iota(jnp.int32, (pairs, 128), 0)
    erow = lax.broadcasted_iota(jnp.int32, (pairs, experts), 1)
    for layer in range(layers):
        ids = jnp.full((pairs, 1), -1, jnp.int32)
        gate = jnp.zeros((pairs, 128), F32)
        for t in range(batch):
            for j in range(top_k):
                kept = jnp.where(slot_s[layer, t, j] >= 0, ids_s[layer, t, j], -1)
                ids = jnp.where(row == t * top_k + j, kept, ids)
                gate = jnp.where(grow == t * top_k + j, rw_s[layer, t, j], gate)
        hot = jnp.where(erow == ids, 1.0, 0.0)
        sel[layer] = hot.astype(BF)
        gates[layer] = gate
        tok = jnp.sum(hot.reshape(batch, top_k, experts), axis=1)
        tok = jnp.concatenate([tok, jnp.zeros((128 - batch, experts), F32)], axis=0)
        place[layer] = tok.T.astype(BF)
    osc[...] = jnp.zeros(osc.shape, F32)

    col = lax.broadcasted_iota(jnp.int32, (heads, seq), 1)
    odd = lax.broadcasted_iota(jnp.int32, (experts, w1.shape[3]), 0) % 2
    resid = jnp.concatenate([xb[...].astype(F32), jnp.zeros((8 - batch, d_model), F32)], axis=0)

    def share(layer):
        def send(i, carry):
            dst = peer(i * cs)
            pltpu.make_async_remote_copy(
                src_ref=pack.at[layer],
                dst_ref=sw.at[layer, :, pl.ds(pl.multiple_of(my_core * half + chip * 2, 2), 2)],
                send_sem=ws_sem.at[layer], recv_sem=wr_sem.at[layer],
                device_id={"dp": dst}, device_id_type=MESH,
            ).start()
            return carry

        lax.fori_loop(1, group // cs, send, 0)
        for i, src in enumerate((w1s_in, w3s_in, w2s_in)):
            own = sw.at[layer, i, pl.ds(pl.multiple_of(my_core * half + chip * 2, 2), 2)]
            pltpu.make_async_copy(src.at[layer], own, wr_sem.at[layer]).start()

    def share_wait(layer):
        part = size.at[pl.ds(0, 3 * (group // cs - 1))]
        pltpu.make_async_remote_copy(
            src_ref=part, dst_ref=part, send_sem=ws_sem.at[layer], recv_sem=wr_sem.at[layer],
            device_id={"dp": me}, device_id_type=MESH,
        ).wait_send()
        part = sw.at[layer, :, pl.ds(0, half)]
        pltpu.make_async_remote_copy(
            src_ref=part, dst_ref=part, send_sem=ws_sem.at[layer], recv_sem=wr_sem.at[layer],
            device_id={"dp": me}, device_id_type=MESH,
        ).wait_recv()

    def forward(layer):
        mine = sw.at[layer, :, pl.ds(pl.multiple_of(my_core * half, 8), half)]
        return pltpu.make_async_remote_copy(
            src_ref=mine, dst_ref=mine, send_sem=fs_sem.at[layer], recv_sem=fr_sem.at[layer],
            device_id={"dp": chip * cs + (cs - 1 - my_core)}, device_id_type=MESH,
        )

    def exchange(src, dst, layer, send_sem, recv_sem):
        def send(i, carry):
            to = peer(i)
            pltpu.make_async_remote_copy(
                src_ref=src.at[layer, pl.ds(pl.multiple_of(to * 2, 2), 2)],
                dst_ref=dst.at[layer, pl.ds(pl.multiple_of(me * 2, 2), 2)],
                send_sem=send_sem.at[layer], recv_sem=recv_sem.at[layer],
                device_id={"dp": to}, device_id_type=MESH,
            ).start()
            return carry

        lax.fori_loop(1, group, send, 0)
        own = pl.ds(pl.multiple_of(me * 2, 2), 2)
        pltpu.make_async_copy(src.at[layer, own], dst.at[layer, own], recv_sem.at[layer]).start()

    def exchange_done(dst, layer, send_sem, recv_sem):
        part = size.at[pl.ds(0, group - 1)]
        pltpu.make_async_remote_copy(
            src_ref=part, dst_ref=part, send_sem=send_sem.at[layer], recv_sem=recv_sem.at[layer],
            device_id={"dp": me}, device_id_type=MESH,
        ).wait_send()
        pltpu.make_async_remote_copy(
            src_ref=dst.at[layer], dst_ref=dst.at[layer], send_sem=send_sem.at[layer], recv_sem=recv_sem.at[layer],
            device_id={"dp": me}, device_id_type=MESH,
        ).wait_recv()

    for layer in range(layers):
        h = rms(resid).astype(BF)
        for c in range(nq):
            q_copy(layer, c).wait()
            qflat[:, c * q_cols:(c + 1) * q_cols] = dot(h, wq[c])
            issue(1)
        for hd in range(heads):
            lo = hd * kv_dim
            base = lo // 128 * 128
            wide = qflat[:, base:base + -(-(lo - base + kv_dim) // 128) * 128]
            qs[hd] = wide[:, lo - base:lo - base + kv_dim]
        if layer == 0:
            pl.semaphore_wait(barrier, group - 1)
            for cp in packs:
                cp.wait()
        share(layer)
        for b in range(batch):
            kv_copy(layer, b).wait()
            s = dot(qs[:, b, :].astype(BF), kv[layer, b]) * ATT_SCALE
            s = jnp.where(col < len_s[b], s, -jnp.inf)
            e = jnp.exp(s - jnp.max(s, axis=-1, keepdims=True))
            p = (e / jnp.sum(e, axis=-1, keepdims=True)).astype(BF)
            osc[b] = nt_dot(p, kv[layer, b, 0:latent, :])
            issue(1)
        acc = jnp.zeros((8, d_model), F32)
        for c in range(no):
            o_copy(layer, c).wait()
            for i in range(o_rows // latent):
                hd = c * (o_rows // latent) + i
                acc += dot(osc[:, hd, :].astype(BF), wo[c, i * latent:(i + 1) * latent])
            issue(1)
        resid = (resid + acc).astype(BF).astype(F32)
        g32 = rms(resid).astype(BF).astype(F32)
        g = g32.astype(BF)
        gpad = jnp.concatenate([g32, jnp.zeros((120, d_model), F32)], axis=0).astype(BF)
        disp_out[layer] = dot(place[layer], gpad).astype(BF)
        exchange(disp_out, disp_in, layer, ds_sem, dr_sem)
        if layer == 0:
            issue(len(stream))
            for cp in [kv_copy(1, b) for b in range(batch)] + ex_copies(1):
                cp.start()
            for c in range(nq):
                q_copy(1, c).start()
            for c in range(no):
                o_copy(1, c).start()
        share_wait(layer)
        fwd = forward(layer)
        fwd.start()
        for cp in ex_copies(layer):
            cp.wait()
        fwd.wait()
        gate_in = nt_dot(g, sw[layer, 1])
        up_in = nt_dot(g, sw[layer, 0])
        shared = dot((jax.nn.silu(gate_in) * up_in).astype(BF), sw[layer, 2])
        exchange_done(disp_in, layer, ds_sem, dr_sem)
        toks = disp_in[layer]
        u = None
        for n in range(2):
            gate_in = dot(toks, w3[layer, n])
            up_in = dot(toks, w1[layer, n])
            hid = jnp.where(odd == n, jax.nn.silu(gate_in) * up_in, 0.0).astype(BF)
            part = dot(hid, w2[layer, n])
            u = part if u is None else u + part
        ret_out[layer] = u.astype(BF)
        exchange(ret_out, ret_in, layer, rs_sem, rr_sem)
        exchange_done(ret_in, layer, rs_sem, rr_sem)
        picked = dot(sel[layer], ret_in[layer])
        gate = gates[layer]
        picked = picked * jnp.concatenate([gate] * (d_model // 128), axis=1)
        routed = jnp.sum(picked.reshape(batch, top_k, d_model), axis=1)
        routed = jnp.concatenate([routed, jnp.zeros((8 - batch, d_model), F32)], axis=0)
        resid = (resid + routed + shared).astype(BF).astype(F32)
    out_ref[...] = resid[0:batch].astype(BF)


def solution(mesh):
    group = mesh.shape['dp']
    tok_axes = ('replica', 'dp')
    in_specs = (
        P(tok_axes, None), P(tok_axes), P(None, tok_axes, None, None),
        P(None, None, None), P(None, None, None),
        P(None, tok_axes, None), P(None, tok_axes, None), P(None, tok_axes, None),
        P(None, 'dp', None, None), P(None, 'dp', None, None), P(None, 'dp', None, None),
        P(None, None, 'dp'), P(None, None, 'dp'), P(None, 'dp', None),
    )

    def device_step(x, lengths, cache, w_q, w_o, expert_ids, slots, route_w, w1_exp, w3_exp, w2_exp, w1_sh, w3_sh, w2_sh):
        batch, d_model = x.shape
        layers, _, seq, kv_dim = cache.shape
        top_k = expert_ids.shape[2]
        experts = w1_exp.shape[1] * group
        heads = w_q.shape[2] // kv_dim
        latent = w_o.shape[1] // heads
        q_cols = 1024 if w_q.shape[2] % 1024 == 0 else 256
        o_rows = 2 * latent
        nq, no = w_q.shape[2] // q_cols, w_o.shape[1] // o_rows
        kv_t = jnp.swapaxes(cache, 2, 3)
        w1s_t = jnp.swapaxes(w1_sh, 1, 2)
        w3s_t = jnp.swapaxes(w3_sh, 1, 2)
        args = (x, lengths, kv_t, w_q, w_o, expert_ids, slots, route_w, w1_exp, w3_exp, w2_exp, w1s_t, w3s_t, w2_sh)
        dma = pltpu.SemaphoreType.DMA
        return pl.pallas_call(
            functools.partial(kernel, group, nq, no),
            out_shape=jax.ShapeDtypeStruct((batch, d_model), BF),
            in_specs=[pl.BlockSpec(memory_space=pl.ANY)] * len(args),
            out_specs=pl.BlockSpec(memory_space=pltpu.VMEM),
            scratch_shapes=[
                pltpu.VMEM((batch, d_model), BF),
                pltpu.SMEM(lengths.shape, jnp.int32),
                pltpu.SMEM(expert_ids.shape, jnp.int32),
                pltpu.SMEM(slots.shape, jnp.int32),
                pltpu.SMEM(route_w.shape, F32),
                pltpu.VMEM(kv_t.shape, BF),
                pltpu.VMEM((nq, d_model, q_cols), BF),
                pltpu.VMEM((no, o_rows, d_model), BF),
                pltpu.VMEM(w1_exp.shape, BF),
                pltpu.VMEM(w3_exp.shape, BF),
                pltpu.VMEM(w2_exp.shape, BF),
                pltpu.VMEM((layers, 3, 2, d_model), BF),
                pltpu.VMEM((layers, 3, 2 * group, d_model), BF),
                pltpu.VMEM((layers, experts, d_model), BF),
                pltpu.VMEM((layers, experts, d_model), BF),
                pltpu.VMEM((layers, experts, d_model), BF),
                pltpu.VMEM((layers, experts, d_model), BF),
                pltpu.VMEM((3 * group // 2, 2, d_model), BF),
                pltpu.VMEM((8, w_q.shape[2]), F32),
                pltpu.VMEM((heads, 8, kv_dim), F32),
                pltpu.VMEM((8, heads, latent), F32),
                pltpu.VMEM((layers, batch * top_k, experts), BF),
                pltpu.VMEM((layers, experts, 128), BF),
                pltpu.VMEM((layers, batch * top_k, 128), F32),
                dma((5,)), dma((layers, batch)), dma((nq,)), dma((no,)), dma((layers, 3)), dma((3,)),
                dma((layers,)), dma((layers,)), dma((layers,)), dma((layers,)),
                dma((layers,)), dma((layers,)), dma((layers,)), dma((layers,)),
            ],
            compiler_params=pltpu.CompilerParams(
                collective_id=0, has_side_effects=True, vmem_limit_bytes=60 * 1024 * 1024
            ),
        )(*args)

    return jax.shard_map(device_step, mesh=mesh, in_specs=in_specs, out_specs=P(tok_axes, None), check_vma=False)
```

time: 462 us -> 76.7 us (0.17)
  waiting for transfers between devices: 277 us -> 0 us
  blocking collectives: 91 us -> 0 us
  Pallas kernels: 0 us -> 75.2 us
  matrix products: 45.5 us -> 0 us
  starting transfers between devices: 22.6 us -> 0 us
  between operations: 13.7 us -> 0.01 us
  local copies, waits for them, and re-layouts: 8.91 us -> 1.29 us
    unnamed x4 -> x0, waiting for transfers between devices: 253 us -> none
    pallas_call x0 -> x1, Pallas kernels: none -> 75.2 us  [device_step(): pl.pallas_call(functools.partial(kernel, group, nq, no), out_shape=jax.Sh...]
    all_gather x2 -> x0, blocking collectives: 73 us -> none  [device_step(): gathered = lax.all_gather(ffn_in, 'dp', axis=0, tiled=True)]
    dot_general x18 -> x0, matrix products: 40.8 us -> none  [the longest x2 16 us: local_attention(): jnp.dot(normed, w_q_l, preferred_element_type=jnp.float32)]
    all_to_all x3 -> x0, waiting for transfers between devices: 23.5 us -> none  [the longest x1 13.3 us: device_step(): returned = lax.all_to_all(expert_out, 'dp', 0, 0, tiled=True)]
    all_to_all x3 -> x0, starting transfers between devices: 22.5 us -> none  [the longest x2 16.9 us: device_step(): recv_buf = lax.all_to_all(send_buf, 'dp', 0, 0, tiled=True)]
    all_to_all x1 -> x0, blocking collectives: 18 us -> none  [device_step(): returned = lax.all_to_all(expert_out, 'dp', 0, 0, tiled=True)]
    sub x2 -> x0, matrix products: 4.7 us -> none  [local_attention(): jax.nn.softmax(jnp.where(valid, scores, -jnp.inf), axis=-1)]
  transfers between devices with their start and end apart: 5 -> 0, of which waited for: 4 -> 0; matrix products, arithmetic and copies ran while one was open for 3% -> 0% of each run, Pallas kernels for 0% -> 0%
where the time goes in v1:
time: 76.7 us; the launch traced here: 76.5 us
  Pallas kernels  75.2 us (98%)
  local copies, waits for them, and re-layouts  1.29 us (2%)
    pallas_call x1, Pallas kernels, device_step(): pl.pallas_call(functools.partial(kernel, group, nq, no), out_shape=jax.Sh...  75.2 us

profile of v1, /device:TPU:1, one launch (start us, length us, event | category | flops | bytes accessed | tf_op | source)
XLA Modules:
  0.0 76.5 jit_solution(13806591754576273649)
XLA Ops:
  0.0 75.2 %shard_map.136 = bf16[4,896]{1,0:T(4,128)(2,1)} custom-call(bf16[4,896]{1,0:T(4,128)(2,1)} %x_in.1, s32[4]{0:T(128)} %len_in.1, bf16[2,4,576,512]{3,2,1,0:T(8,128)(2,1)} %bitcast.3, bf16[2,896,9216]{2,1,0:T(8,128)(2,1)} %wq_in.1, bf16[2,8192,896]{2,1,0:T(8,128)(2,1)} %wo_in.1, s32[2,4,8]{2,1,0:T(4,128)} %ids_in.1, s32[2,4,8]{2,1,0:T(4,128)} %slot_in.1, ...), custom_call_target="tpu_custom_call" | custom-call | tf_op jit(solution)/shard_map/pallas_call | solution.py:303
  75.2 1.3 %copy.16 = bf16[4,896]{1,0:T(4,128)(2,1)} copy(bf16[4,896]{1,0:T(4,128)(2,1)} %shard_map.136) | data formatting | bytes 14336
